TPU v7x, 32 devices: a whole 2x2x4 slice. The times are simulated.
32 devices in a mesh: grp: 8 (over y, x, core), sp: 4 (over z).
Axes of the slice: x: 2, y: 2, z: 4, core: 2. Of those that a mesh axis runs over, the one named last changes fastest.
Arguments:
- latents: bfloat16 [8, 512, 3072], P('grp', 'sp'), may hold values from -6 to 6
- timestep: int32 [8], P('grp'), may hold values from 0 to 999
- w_mod: bfloat16 [256, 9216], replicated, may hold values from -0.375 to 0.375
- w_qkv: bfloat16 [4, 3072, 384], P('sp', 'grp'), may hold values from -2 to 2
- w_out: bfloat16 [4, 128, 3072], P('sp', 'grp'), may hold values from -0.5 to 0.5
Outputs:
- update: bfloat16 [8, 512, 3072], P('grp', 'sp')
All inputs are finite; a program needn't handle non-finite values.
Results may differ from a plain program's by a relative error of at most 0.012.
Values may be sent and summed in bfloat16 or wider, within the bound.
A program may use at most 128 MiB of HBM per device.

v0:
```python
import math
import jax
import jax.numpy as jnp
from jax import lax
from jax.sharding import PartitionSpec as P


def modulation(timestep, w_mod):
    half_freq = w_mod.shape[0] // 2
    freqs = jnp.exp(-math.log(10000.0) * jnp.arange(half_freq, dtype=jnp.float32) / half_freq)
    angles = timestep.astype(jnp.float32)[:, None] * freqs[None, :]
    embed = jnp.concatenate([jnp.cos(angles), jnp.sin(angles)], axis=1).astype(jnp.bfloat16)
    return jnp.dot(embed, w_mod, preferred_element_type=jnp.float32)


def normalize(latents, shift, scale):
    values = latents.astype(jnp.float32)
    center = jnp.mean(values, axis=-1, keepdims=True)
    spread = jnp.mean((values - center) ** 2, axis=-1, keepdims=True)
    normed = (values - center) * lax.rsqrt(spread + 1e-06)
    return (normed * (1.0 + scale[:, None, :]) + shift[:, None, :]).astype(jnp.bfloat16)


def attend(query, keys, values):
    length, head_size = query.shape
    block = min(512, length)
    blocks = query.reshape(length // block, block, head_size)

    def one_block(query_rows):
        scores = lax.dot_general(
            query_rows, keys, (((1,), (1,)), ((), ())), preferred_element_type=jnp.float32
        )
        scores = scores / math.sqrt(head_size)
        largest = jnp.max(scores, axis=1, keepdims=True)
        weights = jnp.exp(scores - largest)
        probs = (weights / jnp.sum(weights, axis=1, keepdims=True)).astype(jnp.bfloat16)
        return jnp.dot(probs, values, preferred_element_type=jnp.float32).astype(jnp.bfloat16)

    return lax.map(one_block, blocks).reshape(length, head_size)


def on_device(latents, timestep, w_mod, w_qkv, w_out):
    images, tok_local, width = latents.shape
    triple = w_qkv.shape[2]
    head_size = triple // 3
    mod = modulation(timestep, w_mod)
    shift = mod[:, :width]
    scale = mod[:, width : 2 * width]
    gate = mod[:, 2 * width :]
    normed = normalize(latents, shift, scale)
    whole = lax.all_gather(normed, "sp", axis=1, tiled=True)
    qkv_sum = jnp.einsum(
        "itc,cf->itf",
        whole,
        lax.all_gather(w_qkv, "grp", axis=1, tiled=True)[0],
        preferred_element_type=jnp.float32,
    )
    qkv = qkv_sum.astype(jnp.bfloat16)
    out_rows = lax.all_gather(w_out, "grp", axis=1, tiled=True)
    attended = jnp.stack(
        [
            attend(
                qkv[0, :, :head_size],
                qkv[0, :, head_size : 2 * head_size],
                qkv[0, :, 2 * head_size :],
            )
        ]
    )
    mine = lax.all_to_all(attended, "sp", split_axis=1, concat_axis=2, tiled=True)
    piece = lax.all_gather(out_rows, "sp", axis=0, tiled=True)
    count = piece.shape[0]
    mixed = mine
    mixed = mixed.reshape(images, tok_local, count, head_size)
    contrib = jnp.einsum("itnc,ncd->itnd", mixed, piece, preferred_element_type=jnp.float32).astype(
        jnp.bfloat16
    )
    contrib = lax.optimization_barrier(contrib)
    total = jnp.sum(contrib.astype(jnp.float32), axis=2)
    return (gate[:, None, :] * total).astype(jnp.bfloat16)


def solution(mesh):
    placed = (P("grp", "sp", None), P("grp"), P(), P("sp", "grp", None), P("sp", "grp", None))
    return jax.shard_map(
        on_device, mesh=mesh, in_specs=placed, out_specs=P("grp", "sp", None), check_vma=False
    )
```

profile of v0, /device:TPU:0, one launch (start us, length us, event | category | flops | bytes accessed | tf_op | source)
XLA Modules:
  0.0 184.8 jit_solution(8514768617609309561)
XLA Ops:
  6.5 0.0 all-gather.6.cloned.1.call-start
  6.5 0.7 all-gather.6.cloned.1.call-update
  7.3 0.0 all-gather.4.cloned.1.call-start
  7.9 0.1 sine_convert_fusion
  8.0 1.3 convert_reduce_fusion.1
  9.4 1.5 fusion.6
  10.9 0.0 copy-start
  10.9 3.1 %fusion.25 = f32[1,9216]{1,0:T(1,128)S(1)} fusion(bf16[256,1]{0,1:T(2,128)(2,1)S(1)} %reshape.111, bf16[256,9216]{1,0:T(8,128)(2,1)} %param.7), kind=kOutput, calls=%fused_computation.37 | convolution fusion | flops 4718592 | bytes 4755968 | tf_op jit(solution)/shard_map/dot_general | solution.py:13
  14.0 0.0 copy-start.1
  14.0 0.0 copy-done
  14.0 1.3 fusion.9
  15.3 0.0 all-gather.4.cloned.1.call-update
  15.3 0.0 all-gather.8.cloned.1.call-start
  15.4 0.0 copy-done.1
  15.4 14.1 %all_gather.14 = bf16[1,128,3072]{2,1,0:T(8,128)(2,1)} all-gather(bf16[1,16,3072]{2,1,0:T(8,128)(2,1)S(1)} %copy-done.1), channel_id=1, replica_groups=mesh['grp'=8,'sp'=4] {'grp'}, dimensions={1}, use_global_device_ids=true | all-gather | bytes 884736 | tf_op jit(solution)/shard_map/all_gather | solution.py:59
  29.5 0.0 all-gather.8.cloned.1.call-update
  29.5 12.9 %all-gather.6.cloned.1.call-done = bf16[1,3072,384]{2,1,0:T(8,128)(2,1)} async-done(((bf16[1,384,384]{2,1,0:T(8,128)(2,1)}), bf16[1,3072,384]{2,1,0:T(8,128)(2,1)}) %all-gather.6.cloned.1.call-update) | async-done | bytes 2359312 | tf_op jit(solution)/shard_map/all_gather | solution.py:55
  42.4 65.0 %all-gather.4.cloned.1.call-done = bf16[1,512,3072]{2,1,0:T(8,128)(2,1)} async-done(((bf16[1,128,3072]{2,1,0:T(8,128)(2,1)}), bf16[1,512,3072]{2,1,0:T(8,128)(2,1)}) %all-gather.4.cloned.1.call-update) | async-done | bytes 3145744 | tf_op jit(solution)/shard_map/all_gather | solution.py:51
  107.4 4.4 %fusion.16 = bf16[1,512,384]{2,1,0:T(8,128)(2,1)S(1)} fusion(bf16[1,3072,384]{2,1,0:T(8,128)(2,1)} %all-gather.6.cloned.1.call-done, bf16[1,512,3072]{2,1,0:T(8,128)(2,1)} %all-gather.4.cloned.1.call-done), kind=kOutput, calls=%fused_computation.18 | convolution fusion | flops 1208156160 | bytes 5898240 | tf_op jit(solution)/shard_map/itc,cf->itf/dot_general | solution.py:52
  111.8 0.3 fusion.24
  112.1 0.2 fusion.22
  112.3 0.4 fusion.21
  112.7 0.2 copy.10
  112.9 0.5 broadcast.81
  113.5 1.4 reduce.3
  114.9 11.8 %all_to_all.15 = bf16[4,2,8192]{2,1,0:T(2,128)(2,1)S(1)} all-to-all(bf16[4,2,8192]{2,1,0:T(2,128)(2,1)S(1)} %reshape.113), channel_id=1, replica_groups=mesh['grp'=8,'sp'=4] {'sp'}, dimensions={0} | all-to-all | bytes 262144 | tf_op jit(solution)/shard_map/all_to_all | solution.py:69
  126.7 0.1 reshape.114
  126.8 47.0 %all-gather.8.cloned.1.call-done = bf16[4,128,3072]{2,1,0:T(8,128)(2,1)} async-done(((bf16[1,128,3072]{2,1,0:T(8,128)(2,1)}), bf16[4,128,3072]{2,1,0:T(8,128)(2,1)}) %all-gather.8.cloned.1.call-update) | async-done | bytes 3145744 | tf_op jit(solution)/shard_map/all_gather | solution.py:70
  173.8 2.9 %fusion = bf16[1,128,4,3072]{3,1,2,0:T(8,128)(2,1)S(1)} fusion(bf16[128,4,128]{2,0,1:T(8,128)(2,1)S(1)} %bitcast.61, bf16[4,128,3072]{2,1,0:T(8,128)(2,1)} %all-gather.8.cloned.1.call-done), kind=kOutput, calls=%fused_computation.2 | convolution fusion | flops 404226048 | bytes 6422528 | tf_op jit(solution)/shard_map/itnc,ncd->itnd/dot_general | solution.py:74
  176.7 0.6 convert_reduce_fusion
  177.3 1.0 fusion.10
  (7 shorter events, 0.1 us)
Async XLA Ops:
  6.5 35.9 %all-gather.6.cloned.1.call-start = ((), (), s32[]{:S(2)}) async-start(), calls=%async_computation.2 | async-start | bytes 2654208 | tf_op jit(solution)/shard_map/all_gather | solution.py:55
  7.3 100.2 %all-gather.4.cloned.1.call-start = ((), (), s32[]{:S(2)}) async-start(), calls=%async_computation.1 | async-start | bytes 3932160 | tf_op jit(solution)/shard_map/all_gather | solution.py:51
  10.9 3.2 %copy-start = (bf16[1,128,3072]{2,1,0:T(8,128)(2,1)S(1)}, bf16[1,128,3072]{2,1,0:T(8,128)(2,1)}, u32[]{:S(2)}) copy-start(bf16[1,128,3072]{2,1,0:T(8,128)(2,1)} %param.5) | copy-start | bytes 2359300
  14.0 1.4 copy-start.1
  15.3 158.5 %all-gather.8.cloned.1.call-start = ((), (), s32[]{:S(2)}) async-start(), calls=%async_computation.3 | async-start | bytes 3932160 | tf_op jit(solution)/shard_map/all_gather | solution.py:70
Sparse Core Ops, SparseCore 0:
  9.2 33.1 all-gather.5
  44.0 63.4 all-gather.3
  109.0 64.7 all-gather.7
where the time goes:
time: 185 us
  waiting for transfers between devices  126 us (68%)
  blocking collectives  25.8 us (14%)
  between operations  13.9 us (8%)
  matrix products  11.1 us (6%)
  other arithmetic  7.36 us (4%)
    all_gather x1, waiting for transfers between devices, on_device(): whole = lax.all_gather(normed, 'sp', axis=1, tiled=True)  65 us
    all_gather x1, waiting for transfers between devices, on_device(): piece = lax.all_gather(out_rows, 'sp', axis=0, tiled=True)  47 us
    all_gather x1, blocking collectives, on_device(): out_rows = lax.all_gather(w_out, 'grp', axis=1, tiled=True)  14.1 us
    all_gather x1, waiting for transfers between devices, on_device(): lax.all_gather(w_qkv, 'grp', axis=1, tiled=True)[0]  12.9 us
    all_to_all x1, blocking collectives, on_device(): lax.all_to_all(attended, 'sp', split_axis=1, concat_axis=2, tiled=True)  11.8 us
    dot_general x1, matrix products, on_device(): jnp.einsum('itc,cf->itf', whole, lax.all_gather(w_qkv, 'grp', axis=1, til...  4.41 us
  transfers between devices with their start and end apart: 3, of which 3 were waited for; matrix products, arithmetic and copies ran while one was open for 8% of the time, Pallas kernels for 0%

commit v1 on v0

--- a/solution.py
+++ b/solution.py
@@ -3,6 +3,11 @@
 import jax.numpy as jnp
 from jax import lax
 from jax.sharding import PartitionSpec as P
+
+
+def stack_and_merge(x, axis, d):
+    parts = lax.all_gather(x, axis)
+    return jnp.concatenate(parts, axis=d)
 
 
 def modulation(timestep, w_mod):
@@ -48,7 +53,7 @@
     scale = mod[:, width : 2 * width]
     gate = mod[:, 2 * width :]
     normed = normalize(latents, shift, scale)
-    whole = lax.all_gather(normed, "sp", axis=1, tiled=True)
+    whole = stack_and_merge(normed, "sp", 1)
     qkv_sum = jnp.einsum(
         "itc,cf->itf",
         whole,

time: 185 us -> 185 us (level)
  no operation moved by 1% of the time
where the time goes in v1:
time: 185 us
  waiting for transfers between devices  126 us (68%)
  blocking collectives  25.8 us (14%)
  between operations  13.9 us (8%)
  matrix products  11.1 us (6%)
  other arithmetic  7.34 us (4%)
    all_gather x1, waiting for transfers between devices, stack_and_merge(): parts = lax.all_gather(x, axis)  65 us
    all_gather x1, waiting for transfers between devices, on_device(): piece = lax.all_gather(out_rows, 'sp', axis=0, tiled=True)  47 us
    all_gather x1, blocking collectives, on_device(): out_rows = lax.all_gather(w_out, 'grp', axis=1, tiled=True)  14.1 us
    all_gather x1, waiting for transfers between devices, on_device(): lax.all_gather(w_qkv, 'grp', axis=1, tiled=True)[0]  12.9 us
    all_to_all x1, blocking collectives, on_device(): lax.all_to_all(attended, 'sp', split_axis=1, concat_axis=2, tiled=True)  11.8 us
    dot_general x1, matrix products, on_device(): jnp.einsum('itc,cf->itf', whole, lax.all_gather(w_qkv, 'grp', axis=1, til...  4.4 us
  transfers between devices with their start and end apart: 3, of which 3 were waited for; matrix products, arithmetic and copies ran while one was open for 8% of the time, Pallas kernels for 0%

profile of v1, /device:TPU:0, one launch (start us, length us, event | category | flops | bytes accessed | tf_op | source)
XLA Modules:
  0.0 184.8 jit_solution(15497897379941692640)
XLA Ops:
  6.5 0.0 all-gather.5.cloned.1.call-start
  6.5 0.7 all-gather.5.cloned.1.call-update
  7.3 0.0 all-gather.9.cloned.1.call-start
  7.9 0.1 sine_convert_fusion
  8.0 1.3 convert_reduce_fusion.1
  9.4 1.5 fusion.5
  10.9 0.0 copy-start
  10.9 3.1 %fusion.20 = f32[1,9216]{1,0:T(1,128)S(1)} fusion(bf16[256,1]{0,1:T(2,128)(2,1)S(1)} %reshape.115, bf16[256,9216]{1,0:T(8,128)(2,1)} %param.7), kind=kOutput, calls=%fused_computation.36 | convolution fusion | flops 4718592 | bytes 4755968 | tf_op jit(solution)/shard_map/dot_general | solution.py:18
  14.0 0.0 copy-start.1
  14.0 0.0 copy-done
  14.0 1.3 fusion.8
  15.3 0.0 all-gather.9.cloned.1.call-update
  15.3 0.0 all-gather.7.cloned.1.call-start
  15.4 0.0 copy-done.1
  15.4 14.1 %all_gather.18 = bf16[1,128,3072]{2,1,0:T(8,128)(2,1)} all-gather(bf16[1,16,3072]{2,1,0:T(8,128)(2,1)S(1)} %copy-done.1), channel_id=1, replica_groups=mesh['grp'=8,'sp'=4] {'grp'}, dimensions={1}, use_global_device_ids=true | all-gather | bytes 884736 | tf_op jit(solution)/shard_map/all_gather | solution.py:64
  29.5 0.0 all-gather.7.cloned.1.call-update
  29.5 12.9 %all-gather.5.cloned.1.call-done = bf16[1,3072,384]{2,1,0:T(8,128)(2,1)} async-done(((bf16[1,384,384]{2,1,0:T(8,128)(2,1)}), bf16[1,3072,384]{2,1,0:T(8,128)(2,1)}) %all-gather.5.cloned.1.call-update) | async-done | bytes 2359312 | tf_op jit(solution)/shard_map/all_gather | solution.py:60
  42.4 65.0 %all-gather.9.cloned.1.call-done = bf16[4,128,3072]{2,1,0:T(8,128)(2,1)} async-done(((bf16[1,128,3072]{2,1,0:T(8,128)(2,1)}), bf16[4,128,3072]{2,1,0:T(8,128)(2,1)}) %all-gather.9.cloned.1.call-update) | async-done | bytes 3145744 | tf_op jit(solution)/shard_map/all_gather | solution.py:9
  107.4 4.4 %fusion.13 = bf16[1,512,384]{2,1,0:T(8,128)(2,1)S(1)} fusion(bf16[512,3072]{1,0:T(8,128)(2,1)} %bitcast.60, bf16[1,3072,384]{2,1,0:T(8,128)(2,1)} %all-gather.5.cloned.1.call-done), kind=kOutput, calls=%fused_computation.17 | convolution fusion | flops 1208156160 | bytes 5898240 | tf_op jit(solution)/shard_map/itc,cf->itf/dot_general | solution.py:57
  111.8 0.3 fusion.19
  112.2 0.2 fusion.17
  112.4 0.4 fusion.16
  112.7 0.2 copy.10
  113.0 0.5 broadcast.81
  113.5 1.4 reduce.3
  114.9 11.8 %all_to_all.15 = bf16[4,2,8192]{2,1,0:T(2,128)(2,1)S(1)} all-to-all(bf16[4,2,8192]{2,1,0:T(2,128)(2,1)S(1)} %reshape.117), channel_id=1, replica_groups=mesh['grp'=8,'sp'=4] {'sp'}, dimensions={0} | all-to-all | bytes 262144 | tf_op jit(solution)/shard_map/all_to_all | solution.py:74
  126.7 0.1 reshape.118
  126.8 47.0 %all-gather.7.cloned.1.call-done = bf16[4,128,3072]{2,1,0:T(8,128)(2,1)} async-done(((bf16[1,128,3072]{2,1,0:T(8,128)(2,1)}), bf16[4,128,3072]{2,1,0:T(8,128)(2,1)}) %all-gather.7.cloned.1.call-update) | async-done | bytes 3145744 | tf_op jit(solution)/shard_map/all_gather | solution.py:75
  173.9 2.9 %fusion = bf16[1,128,4,3072]{3,1,2,0:T(8,128)(2,1)S(1)} fusion(bf16[128,4,128]{2,0,1:T(8,128)(2,1)S(1)} %bitcast.56, bf16[4,128,3072]{2,1,0:T(8,128)(2,1)} %all-gather.7.cloned.1.call-done), kind=kOutput, calls=%fused_computation.2 | convolution fusion | flops 404226048 | bytes 6422528 | tf_op jit(solution)/shard_map/itnc,ncd->itnd/dot_general | solution.py:79
  176.7 0.6 convert_reduce_fusion
  177.3 1.0 fusion.9
  (7 shorter events, 0.1 us)
Async XLA Ops:
  6.5 35.9 %all-gather.5.cloned.1.call-start = ((), (), s32[]{:S(2)}) async-start(), calls=%async_computation.1 | async-start | bytes 2654208 | tf_op jit(solution)/shard_map/all_gather | solution.py:60
  7.3 100.2 %all-gather.9.cloned.1.call-start = ((), (), s32[]{:S(2)}) async-start(), calls=%async_computation.3 | async-start | bytes 3932160 | tf_op jit(solution)/shard_map/all_gather | solution.py:9
  10.9 3.2 %copy-start = (bf16[1,128,3072]{2,1,0:T(8,128)(2,1)S(1)}, bf16[1,128,3072]{2,1,0:T(8,128)(2,1)}, u32[]{:S(2)}) copy-start(bf16[1,128,3072]{2,1,0:T(8,128)(2,1)} %param.5) | copy-start | bytes 2359300
  14.0 1.4 copy-start.1
  15.3 158.5 %all-gather.7.cloned.1.call-start = ((), (), s32[]{:S(2)}) async-start(), calls=%async_computation.2 | async-start | bytes 3932160 | tf_op jit(solution)/shard_map/all_gather | solution.py:75
Sparse Core Ops, SparseCore 0:
  9.2 33.1 all-gather.4
  44.0 63.4 all-gather.8
  109.0 64.7 all-gather.6
